TPU v7x, 128 devices: a whole 4x4x4 slice. The times are simulated.
128 devices in a mesh: row: 8 (over z, x_lo), col: 16 (over x_hi, y, core).
Axes of the slice: x: 4 (x_hi: 2, x_lo: 2; x = x_hi * 2 + x_lo), y: 4, z: 4, core: 2. Of those that a mesh axis runs over, the one named last changes fastest.
Arguments:
- occupations: int32 [8192, 128], P('row'), may hold values from 0 to 2
- table: float32 [384, 1024], replicated, may hold values from -0.5 to 0.5
- weights: float32 [2, 1024, 4096], P(None, None, 'col'), may hold values from -0.1875 to 0.1875
- biases: float32 [2, 4096], P(None, 'col'), may hold values from -6 to 6
- heads: float32 [2, 4096], P(None, 'col'), may hold values from -18 to 18
- energies: float32 [8192], P('row'), may hold values from -6 to 6
Outputs:
- schur: float32 [8192, 8192], P('row', 'col')
- solved_rhs: float32 [8192], P('row')
All inputs are finite; a program needn't handle non-finite values.
Results may differ from a plain program's by a relative error of at most 0.0034.
Values may be sent and summed in bfloat16 or wider, within the bound.
No kernel may reach another device: no remote copies, remote signals or barrier semaphores. Data moves between devices by JAX's collectives and lax.ppermute only.
A program may use at most 128 MiB of HBM per device.

v0:
```python
import functools
import math
import jax
import jax.numpy as jnp
from jax import lax
from jax.sharding import Mesh
from jax.sharding import PartitionSpec as P

ROW = ("row_0", "row_1")
norm_eps = 1e-06
diag_shift = 0.05


def over_axes(shard, axes):
    return functools.reduce(lax.psum, axes, shard)


def rows_for(lines, devices):
    spare = -len(lines) % devices
    return jnp.pad(lines, [(0, spare)] + [(0, 0)] * (lines.ndim - 1))


def broadcast_by_parts(shard, axis, root):
    lines = jnp.where(lax.axis_index(axis) == root, shard, jnp.zeros_like(shard)).reshape(
        -1, *shard.shape[1:][-1:]
    )
    padded = rows_for(lines, lax.axis_size(axis))
    own = lax.psum_scatter(padded, axis, scatter_dimension=0, tiled=True)
    return lax.all_gather(own, axis, axis=0, tiled=True)[: len(lines)].reshape(shard.shape)


def broadcast(block, axis, holder):
    block = jnp.where(lax.axis_index(axis) == holder, block, jnp.zeros_like(block))
    return lax.psum(block, axis)


def jacobian(occupations, table, weights, biases, heads):
    onehot = jnp.concatenate(
        [
            (occupations == 0).astype(jnp.float32),
            (occupations == 1).astype(jnp.float32),
            (occupations == 2).astype(jnp.float32),
        ],
        axis=1,
    )
    embedded = jnp.dot(
        onehot, table, precision=lax.Precision.HIGHEST, preferred_element_type=jnp.float32
    )
    embedded = embedded * lax.rsqrt(
        jnp.mean(embedded * embedded, axis=-1, keepdims=True) + norm_eps
    )
    blocks = []
    for panel_index in range(2):
        hidden = (
            jnp.dot(
                embedded,
                weights[panel_index],
                precision=lax.Precision.HIGHEST,
                preferred_element_type=jnp.float32,
            )
            + biases[panel_index]
        )
        blocks.append(heads[panel_index] * jax.nn.sigmoid(hidden))
    return jnp.concatenate(blocks, axis=1)


def on_device(occupations, table, weights, biases, heads, energies):
    row_count = occupations.shape[0]
    row_devices = lax.axis_size(ROW)
    col_devices = lax.axis_size("col")
    sample_total = row_count * row_devices
    panel_width = sample_total // col_devices
    derivs = jacobian(occupations, table, weights, biases, heads)
    col_sums = over_axes(jnp.sum(derivs, axis=0), ROW)
    centered = ((derivs - col_sums / sample_total) * (1.0 / math.sqrt(sample_total))).astype(
        jnp.bfloat16
    )
    own_rows = lax.all_gather(centered, "col", axis=1, tiled=True)
    every_sample = lax.all_gather(centered, ROW, axis=0, tiled=True)
    partner = lax.all_to_all(every_sample, "col", split_axis=0, concat_axis=1, tiled=True)
    kernel = lax.dot_general(
        own_rows, partner, (((1,), (1,)), ((), ())), preferred_element_type=jnp.float32
    )
    row_ids = lax.axis_index(ROW) * row_count + lax.iota(jnp.int32, row_count)
    col_ids = lax.axis_index("col") * panel_width + lax.iota(jnp.int32, panel_width)
    kernel = kernel + jnp.where(row_ids[:, None] == col_ids[None, :], diag_shift, 0.0).astype(
        jnp.float32
    )
    right_side = energies
    for panel_index in range(2):
        start_global = panel_index * panel_width
        root_row = start_global // row_count
        offset = start_global % row_count
        top_block, top_side = (
            broadcast_by_parts(kernel[offset : offset + panel_width], ROW, root_row),
            broadcast_by_parts(right_side[offset : offset + panel_width], ROW, root_row),
        )
        column, diag_block = (
            broadcast(kernel, "col", panel_index),
            broadcast(top_block, "col", panel_index),
        )
        factor = jnp.linalg.cholesky(diag_block)
        left_rows = lax.linalg.triangular_solve(
            factor, column, left_side=False, lower=True, transpose_a=True
        )
        right_rows = lax.linalg.triangular_solve(
            factor, top_block.T, left_side=False, lower=True, transpose_a=True
        )
        kernel = kernel - lax.dot_general(
            left_rows,
            right_rows,
            (((1,), (1,)), ((), ())),
            precision=lax.Precision.HIGHEST,
            preferred_element_type=jnp.float32,
        )
        solved = lax.linalg.triangular_solve(factor, top_side[:, None], left_side=True, lower=True)[
            :, 0
        ]
        right_side = right_side - jnp.dot(
            left_rows, solved, precision=lax.Precision.HIGHEST, preferred_element_type=jnp.float32
        )
        placed = right_side.at[offset : offset + panel_width].set(solved)
        right_side = jnp.where(lax.axis_index(ROW) == root_row, placed, right_side)
    return (kernel, right_side)


def solution(mesh):
    torus = Mesh(mesh.devices.reshape(4, 2, mesh.shape["col"]), ("row_0", "row_1", "col"))
    placed = (P(ROW, None), P(), P(None, None, "col"), P(None, "col"), P(None, "col"), P(ROW))
    return jax.shard_map(
        on_device, mesh=torus, in_specs=placed, out_specs=(P(ROW, "col"), P(ROW)), check_vma=False
    )
```

profile of v0, /device:TPU:1, one launch (start us, length us, event | category | flops | bytes accessed | tf_op | source)
XLA Modules:
  0.0 1241.6 jit_solution(15039333910361492338)
XLA Ops:
  8.7 3.6 multiply_reduce_fusion
  12.5 4.2 fusion.58
  16.6 4.4 fusion.52
  21.2 10.6 psum.42
  31.8 3.8 psum.43
  37.5 169.9 %all-gather.7.cloned.1.call-done = bf16[8192,512]{0,1:T(8,128)(2,1)} async-done(((bf16[1024,512]{0,1:T(8,128)(2,1)}), bf16[8192,512]{0,1:T(8,128)(2,1)}) %all-gather.7.cloned.1.call-update) | async-done | bytes 8388624 | tf_op jit(solution)/shard_map/all_gather | solution.py:79
  207.4 7.5 copy.55
  214.9 7.3 all-to-all-start
  222.3 137.7 %all-to-all-done = bf16[16,512,512]{1,2,0:T(8,128)(2,1)} async-done(((bf16[16,512,512]{1,2,0:T(8,128)(2,1)}), bf16[16,512,512]{1,2,0:T(8,128)(2,1)}, u32[]{:S(2)}, u32[]{:S(2)}) %all-to-all-start) | async-done | bytes 8388640 | tf_op jit(solution)/shard_map/all_to_all | solution.py:80
  360.0 54.5 %all-gather.5.cloned.1.call-done = bf16[1024,8192]{0,1:T(8,128)(2,1)} async-done(((bf16[1024,512]{0,1:T(8,128)(2,1)}), bf16[1024,8192]{0,1:T(8,128)(2,1)}) %all-gather.5.cloned.1.call-update) | async-done | bytes 16777232 | tf_op jit(solution)/shard_map/all_gather | solution.py:78
  414.5 15.9 %broadcast_select_fusion.1 = (f32[1024,512]{0,1:T(8,128)}, f32[1024,512]{0,1:T(8,128)S(1)}) fusion(pred[]{:T(512)S(6)} %eq.56, s32[512]{0:T(512)S(1)} %iota_add_fusion.1, s32[1024]{0:T(1024)S(1)} %iota_add_fusion, bf16[1024,8192]{0,1:T(8,128)(2,1)} %all-gather.5.cloned.1.call-done, bf16[512,8192]{0,1:T(8,128)(2,1)} %bitcast.7), kind=kOutput, calls=%fused_computation.126 | convolution fusion | flops 8592031744 | bytes 29366272 | tf_op jit(solution)/shard_map/dot_general | solution.py:81
  433.2 36.6 %reduce-scatter.7.cloned.1.call-done = f32[64,512]{1,0:T(8,128)} async-done(((f32[512,512]{1,0:T(8,128)}), f32[64,512]{1,0:T(8,128)}) %reduce-scatter.7.cloned.1.call-update) | async-done | bytes 131088 | tf_op jit(solution)/shard_map/reduce_scatter | solution.py:28
  469.9 40.9 %all-gather.9.cloned.1.call-done = f32[512,512]{1,0:T(8,128)} async-done(((f32[64,512]{1,0:T(8,128)}), f32[512,512]{1,0:T(8,128)}) %all-gather.9.cloned.1.call-update) | async-done | bytes 1048592 | tf_op jit(solution)/shard_map/all_gather | solution.py:29
  513.8 151.1 %all-reduce.12.cloned.1.call-done = (f32[1024,512]{0,1:T(8,128)}, f32[512,512]{0,1:T(8,128)}) async-done(((f32[1024,512]{0,1:T(8,128)}, f32[512,512]{0,1:T(8,128)}), (f32[1024,512]{0,1:T(8,128)}, f32[512,512]{0,1:T(8,128)})) %all-reduce.12.cloned.1.call-update) | async-done | bytes 3145744 | tf_op jit(solution)/shard_map/psum | solution.py:34
  664.9 2.6 copy.25
  669.9 11.7 cholesky.286
  681.8 9.8 custom-call.35
  694.2 11.7 cholesky.305
  705.9 10.2 custom-call.36
  717.7 11.7 cholesky.326
  730.1 9.8 custom-call.37
  741.4 11.7 cholesky.343
  758.4 11.4 while.14
  759.0 2.2 bitcast_dynamic-update-slice_fusion.4
  761.9 2.2 bitcast_dynamic-update-slice_fusion.4
  764.8 2.2 bitcast_dynamic-update-slice_fusion.4
  769.8 39.3 %custom-call.38 = f32[4,128,128]{1,2,0:T(8,128)S(1)} custom-call(f32[4,128,128]{2,1,0:T(8,128)S(1)} %get-tuple-element.72), custom_call_target="InvertDiagBlocksLowerTriangular" | custom-call | tf_op jit(solution)/shard_map/triangular_solve/custom-call.3 | solution.py:103
  821.3 5.3 broadcast_select_fusion
  829.5 38.3 %reduce-scatter.9.cloned.1.call-done = f32[64,512]{1,0:T(8,128)} async-done(((f32[512,512]{1,0:T(8,128)}), f32[64,512]{1,0:T(8,128)}) %reduce-scatter.9.cloned.1.call-update) | async-done | bytes 131088 | tf_op jit(solution)/shard_map/reduce_scatter | solution.py:28
  867.8 41.0 %all-gather.11.cloned.1.call-done = f32[512,512]{1,0:T(8,128)} async-done(((f32[64,512]{1,0:T(8,128)}), f32[512,512]{1,0:T(8,128)}) %all-gather.11.cloned.1.call-update) | async-done | bytes 1048592 | tf_op jit(solution)/shard_map/all_gather | solution.py:29
  914.0 14.5 %all-reduce.3 = f32[512]{0:T(512)S(1)} all-reduce(f32[512]{0:T(512)S(1)} %slice_select_fusion.3), channel_id=4, replica_groups=mesh['row_0'=4,'row_1'=2,'col'=16] {'row_0','row_1'}, use_global_device_ids=true, to_apply=%region_18.22.clone | all-reduce | flops 512 | bytes 4096
  928.7 12.9 %all-reduce.1 = f32[512]{0:T(512)S(1)} all-reduce(f32[512]{0:T(512)S(1)} %dynamic-slice_dynamic-update-slice_fusion.1), channel_id=1, replica_groups=mesh['row_0'=4,'row_1'=2,'col'=16] {'row_0','row_1'}, use_global_device_ids=true, to_apply=%add.1 | all-reduce | flops 512 | bytes 4096
  943.0 2.4 fusion.68
  945.5 14.7 %all-reduce.4 = f32[512]{0:T(512)S(1)} all-reduce(f32[512]{0:T(512)S(1)} %slice_select_fusion.2), channel_id=5, replica_groups=mesh['row_0'=4,'row_1'=2,'col'=16] {'row_0','row_1'}, use_global_device_ids=true, to_apply=%region_19.24.clone | all-reduce | flops 512 | bytes 4096
  960.4 13.8 %all-reduce.2 = f32[512]{0:T(512)S(1)} all-reduce(f32[512]{0:T(512)S(1)} %dynamic-slice_dynamic-update-slice_fusion), channel_id=1, replica_groups=mesh['row_0'=4,'row_1'=2,'col'=16] {'row_0','row_1'}, use_global_device_ids=true, to_apply=%add.2 | all-reduce | flops 512 | bytes 4096
  974.2 89.2 %all-reduce.10.cloned.1.call-done = (f32[1024,512]{0,1:T(8,128)}, f32[512,512]{0,1:T(8,128)}) async-done(((f32[1024,512]{0,1:T(8,128)}, f32[512,512]{0,1:T(8,128)}), (f32[1024,512]{0,1:T(8,128)}, f32[512,512]{0,1:T(8,128)})) %all-reduce.10.cloned.1.call-update) | async-done | bytes 3145744 | tf_op jit(solution)/shard_map/psum | solution.py:34
  1063.5 2.6 copy.33
  1068.5 11.7 cholesky.358
  1080.4 9.8 custom-call.40
  1092.7 11.7 cholesky.377
  1105.8 10.0 custom-call.41
  1117.3 11.7 cholesky.398
  1129.8 9.8 custom-call.42
  1141.1 11.7 cholesky.415
  1157.3 11.4 while.15
  1168.7 39.3 %custom-call.43 = f32[4,128,128]{1,2,0:T(8,128)S(1)} custom-call(f32[4,128,128]{2,1,0:T(8,128)S(1)} %get-tuple-element.74), custom_call_target="InvertDiagBlocksLowerTriangular" | custom-call | tf_op jit(solution)/shard_map/triangular_solve/custom-call.3 | solution.py:103
  1225.6 5.3 convolution_subtract_fusion
  1230.9 2.9 copy.39
  (197 shorter events, 87.8 us)
Async XLA Ops:
  7.2 1.6 copy-start
  7.2 200.3 %all-gather.7.cloned.1.call-start = ((), (), s32[]{:S(2)}) async-start(), calls=%async_computation.4 | async-start | bytes 9437184 | tf_op jit(solution)/shard_map/all_gather | solution.py:79
  8.7 3.7 copy-start.19
  8.7 3.7 copy-start.20
  8.7 3.7 copy-start.21
  36.8 377.7 %all-gather.5.cloned.1.call-start = ((), (), s32[]{:S(2)}) async-start(), calls=%async_computation.3 | async-start | bytes 17825792 | tf_op jit(solution)/shard_map/all_gather | solution.py:78
  214.9 145.1 %all-to-all-start = ((bf16[16,512,512]{1,2,0:T(8,128)(2,1)}), bf16[16,512,512]{1,2,0:T(8,128)(2,1)}, u32[]{:S(2)}, u32[]{:S(2)}) async-start(bf16[16,512,512]{1,2,0:T(8,128)(2,1)} %bitcast.258), calls=%async_computation | async-start | bytes 16777216 | tf_op jit(solution)/shard_map/all_to_all | solution.py:80
  222.2 247.7 %reduce-scatter.7.cloned.1.call-start = ((), (), s32[]{:S(2)}) async-start(), calls=%async_computation.7 | async-start | bytes 1179648 | tf_op jit(solution)/shard_map/reduce_scatter | solution.py:28
  430.4 1.4 copy-start.6
  433.1 77.7 %all-gather.9.cloned.1.call-start = ((), (), s32[]{:S(2)}) async-start(), calls=%async_computation.5 | async-start | bytes 1179648 | tf_op jit(solution)/shard_map/all_gather | solution.py:29
  469.9 195.0 %all-reduce.12.cloned.1.call-start = ((), (), s32[]{:S(2)}) async-start(), calls=%async_computation.10 | async-start | bytes 6291456 | tf_op jit(solution)/shard_map/psum | solution.py:34
  513.5 354.2 %reduce-scatter.9.cloned.1.call-start = ((), (), s32[]{:S(2)}) async-start(), calls=%async_computation.8 | async-start | bytes 1179648 | tf_op jit(solution)/shard_map/reduce_scatter | solution.py:28
  664.9 2.6 copy-start.10
  669.0 1.0 copy-start.12
  769.8 43.5 %copy-start.4 = (f32[512,512]{1,0:T(8,128)S(1)}, f32[512,512]{1,0:T(8,128)}, u32[]{:S(2)}) copy-start(f32[512,512]{1,0:T(8,128)} %get-tuple-element.260) | copy-start | bytes 3145732
  809.1 4.2 copy-start.15
  814.6 6.6 copy-start.8
  816.4 4.8 copy-start.13
  817.5 3.8 copy-start.7
  826.6 1.4 copy-start.2
  829.4 79.4 %all-gather.11.cloned.1.call-start = ((), (), s32[]{:S(2)}) async-start(), calls=%async_computation.6 | async-start | bytes 1179648 | tf_op jit(solution)/shard_map/all_gather | solution.py:29
  867.8 195.7 %all-reduce.10.cloned.1.call-start = ((), (), s32[]{:S(2)}) async-start(), calls=%async_computation.9 | async-start | bytes 6291456 | tf_op jit(solution)/shard_map/psum | solution.py:34
  911.5 0.7 copy-start.18
  911.5 2.5 copy-start.16
  1063.5 2.6 copy-start.9
  1067.5 1.0 copy-start.11
  1210.5 5.8 copy-start.5
  1210.5 5.8 copy-start.14
  1221.8 3.8 copy-start.3
  1225.6 8.8 copy-start.1
  1233.8 0.6 copy-start.17
Sparse Core Ops, SparseCore 0:
  36.9 170.4 all-gather.6
  210.5 203.9 all-gather.4
  433.3 36.5 reduce-scatter.6
  471.3 39.4 all-gather.8
  513.8 151.0 all-reduce.11
  829.6 38.1 reduce-scatter.8
  869.4 39.4 all-gather.10
  912.0 151.3 all-reduce.9
where the time goes:
time: 1250 us; the launch traced here: 1240 us
  waiting for transfers between devices  760 us (61%)
  other arithmetic  247 us (20%)
  matrix products  82.7 us (7%)
  blocking collectives  70.3 us (6%)
  local copies, waits for them, and re-layouts  51.3 us (4%)
  between operations  21.7 us (2%)
    psum x2, waiting for transfers between devices, broadcast(): return lax.psum(block, axis)  240 us
    all_gather x1, waiting for transfers between devices, on_device(): every_sample = lax.all_gather(centered, ROW, axis=0, tiled=True)  170 us
    another operation x29, other arithmetic, on_device(): factor = jnp.linalg.cholesky(diag_block)  158 us
    all_to_all x1, waiting for transfers between devices, on_device(): lax.all_to_all(every_sample, 'col', split_axis=0, concat_axis=1, tiled=True)  138 us
    all_gather x2, waiting for transfers between devices, broadcast_by_parts(): lax.all_gather(own, axis, axis=0, tiled=True)[:len(lines)]  81.9 us
    another operation x5, other arithmetic, on_device(): lax.linalg.triangular_solve(factor, column, left_side=False, lower=True,...  81.2 us
    reduce_scatter x2, waiting for transfers between devices, broadcast_by_parts(): own = lax.psum_scatter(padded, axis, scatter_dimension=0, tiled=True)  74.9 us
    unnamed x4, blocking collectives  56 us
  transfers between devices with their start and end apart: 9, of which 9 were waited for; matrix products, arithmetic and copies ran while one was open for 1% of the time, Pallas kernels for 0%

commit v1 on v0

--- a/solution.py
+++ b/solution.py
@@ -76,7 +76,9 @@
         jnp.bfloat16
     )
     own_rows = lax.all_gather(centered, "col", axis=1, tiled=True)
-    every_sample = lax.all_gather(centered, ROW, axis=0, tiled=True)
+    every_sample = jnp.concatenate(
+        lax.all_to_all(jnp.stack([centered] * lax.axis_size(ROW)), ROW, 0, 0), axis=0
+    )
     partner = lax.all_to_all(every_sample, "col", split_axis=0, concat_axis=1, tiled=True)
     kernel = lax.dot_general(
         own_rows, partner, (((1,), (1,)), ((), ())), preferred_element_type=jnp.float32

time: 1250 us -> 1180 us (0.944)
  waiting for transfers between devices: 760 us -> 524 us
  blocking collectives: 70.3 us -> 221 us
    all_gather x1 -> x0, waiting for transfers between devices: 170 us -> none  [on_device(): every_sample = lax.all_gather(centered, ROW, axis=0, tiled=True)]
    all_to_all x0 -> x1, blocking collectives: none -> 151 us  [on_device(): lax.all_to_all(jnp.stack([centered] * lax.axis_size(ROW)), ROW, 0, 0)]
    all_gather x1, waiting for transfers between devices: 54.5 us -> 0.01 us  [on_device(): own_rows = lax.all_gather(centered, 'col', axis=1, tiled=True)]
    all_to_all x1, waiting for transfers between devices: 138 us -> 120 us  [on_device(): lax.all_to_all(every_sample, 'col', split_axis=0, concat_axis=1, tiled=True)]
  transfers between devices with their start and end apart: 9 -> 8, of which waited for: 9 -> 7; matrix products, arithmetic and copies ran while one was open for 1% -> 2% of each run, Pallas kernels for 0% -> 0%
where the time goes in v1:
time: 1180 us; the launch traced here: 1170 us
  waiting for transfers between devices  524 us (44%)
  other arithmetic  247 us (21%)
  blocking collectives  221 us (19%)
  matrix products  82.7 us (7%)
  local copies, waits for them, and re-layouts  58.4 us (5%)
  between operations  21.7 us (2%)
  starting transfers between devices  12.1 us (1%)
    psum x2, waiting for transfers between devices, broadcast(): return lax.psum(block, axis)  240 us
    another operation x29, other arithmetic, on_device(): factor = jnp.linalg.cholesky(diag_block)  158 us
    all_to_all x1, blocking collectives, on_device(): lax.all_to_all(jnp.stack([centered] * lax.axis_size(ROW)), ROW, 0, 0)  151 us
    all_to_all x1, waiting for transfers between devices, on_device(): lax.all_to_all(every_sample, 'col', split_axis=0, concat_axis=1, tiled=True)  120 us
    all_gather x2, waiting for transfers between devices, broadcast_by_parts(): lax.all_gather(own, axis, axis=0, tiled=True)[:len(lines)]  81.9 us
    reduce_scatter x2, waiting for transfers between devices, broadcast_by_parts(): own = lax.psum_scatter(padded, axis, scatter_dimension=0, tiled=True)  81.5 us
    another operation x5, other arithmetic, on_device(): lax.linalg.triangular_solve(factor, column, left_side=False, lower=True,...  81.2 us
    unnamed x4, blocking collectives  56 us
  transfers between devices with their start and end apart: 8, of which 7 were waited for; matrix products, arithmetic and copies ran while one was open for 2% of the time, Pallas kernels for 0%

profile of v1, /device:TPU:1, one launch (start us, length us, event | category | flops | bytes accessed | tf_op | source)
XLA Modules:
  0.0 1167.3 jit_solution(15369498677767221358)
XLA Ops:
  8.7 3.6 multiply_reduce_fusion
  12.5 4.2 fusion.58
  16.6 4.4 fusion.52
  21.2 10.6 psum.42
  31.8 3.8 psum.43
  39.0 150.7 %all_to_all.24 = bf16[8,1024,512]{2,1,0:T(8,128)(2,1)} all-to-all(bf16[8,1024,512]{2,1,0:T(8,128)(2,1)S(1)} %stack.2), channel_id=1, replica_groups=mesh['row_0'=4,'row_1'=2,'col'=16] {'row_0','row_1'}, dimensions={0} | all-to-all | bytes 16777216 | tf_op jit(solution)/shard_map/all_to_all | solution.py:80
  189.7 11.7 all-to-all-start.1
  201.4 119.9 %all-to-all-done.1 = bf16[16,512,512]{2,1,0:T(8,128)(2,1)} async-done(((bf16[16,512,512]{2,1,0:T(8,128)(2,1)}), bf16[16,512,512]{2,1,0:T(8,128)(2,1)}, u32[]{:S(2)}, u32[]{:S(2)}) %all-to-all-start.1) | async-done | bytes 8388640 | tf_op jit(solution)/shard_map/all_to_all | solution.py:82
  321.3 12.3 %copy.37 = bf16[512,16,512]{0,2,1:T(8,128)(2,1)} copy(bf16[512,16,512]{2,0,1:T(8,128)(2,1)} %bitcast.7) | data formatting | bytes 16777216 | tf_op jit(solution)/shard_map/all_to_all | solution.py:82
  333.6 15.9 %broadcast_select_fusion.1 = (f32[1024,512]{0,1:T(8,128)}, f32[1024,512]{0,1:T(8,128)S(1)}) fusion(pred[]{:T(512)S(6)} %eq.56, s32[512]{0:T(512)S(1)} %iota_add_fusion.1, s32[1024]{0:T(1024)S(1)} %iota_add_fusion, bf16[1024,8192]{0,1:T(8,128)(2,1)} %all-gather.4.cloned.1.call-done, bf16[512,8192]{0,1:T(8,128)(2,1)} %bitcast.271), kind=kOutput, calls=%fused_computation.125 | convolution fusion | flops 8592031744 | bytes 29366272 | tf_op jit(solution)/shard_map/dot_general | solution.py:83
  352.3 43.2 %reduce-scatter.7.cloned.1.call-done = f32[64,512]{1,0:T(8,128)} async-done(((f32[512,512]{1,0:T(8,128)}), f32[64,512]{1,0:T(8,128)}) %reduce-scatter.7.cloned.1.call-update) | async-done | bytes 131088 | tf_op jit(solution)/shard_map/reduce_scatter | solution.py:28
  395.6 41.0 %all-gather.6.cloned.1.call-done = f32[512,512]{1,0:T(8,128)} async-done(((f32[64,512]{1,0:T(8,128)}), f32[512,512]{1,0:T(8,128)}) %all-gather.6.cloned.1.call-update) | async-done | bytes 1048592 | tf_op jit(solution)/shard_map/all_gather | solution.py:29
  439.6 151.1 %all-reduce.12.cloned.1.call-done = (f32[1024,512]{0,1:T(8,128)}, f32[512,512]{0,1:T(8,128)}) async-done(((f32[1024,512]{0,1:T(8,128)}, f32[512,512]{0,1:T(8,128)}), (f32[1024,512]{0,1:T(8,128)}, f32[512,512]{0,1:T(8,128)})) %all-reduce.12.cloned.1.call-update) | async-done | bytes 3145744 | tf_op jit(solution)/shard_map/psum | solution.py:34
  590.7 2.6 copy.41
  595.8 11.7 %cholesky.286 = f32[128,128]{1,0:T(8,128)S(1)} custom-call(f32[128,128]{1,0:T(8,128)S(1)} %cholesky.426), custom_call_target="Cholesky" | custom-call | tf_op jit(solution)/shard_map/jit(cholesky)/cholesky | solution.py:104
  607.7 9.8 custom-call.35
  620.0 11.7 %cholesky.305 = f32[128,128]{1,0:T(8,128)S(1)} custom-call(f32[128,128]{1,0:T(8,128)S(1)} %cholesky.430), custom_call_target="Cholesky" | custom-call | tf_op jit(solution)/shard_map/jit(cholesky)/cholesky | solution.py:104
  631.8 10.2 custom-call.36
  643.6 11.7 %cholesky.326 = f32[128,128]{1,0:T(8,128)S(1)} custom-call(f32[128,128]{1,0:T(8,128)S(1)} %cholesky.435), custom_call_target="Cholesky" | custom-call | tf_op jit(solution)/shard_map/jit(cholesky)/cholesky | solution.py:104
  656.0 9.8 custom-call.37
  667.2 11.7 %cholesky.343 = f32[128,128]{1,0:T(8,128)S(1)} custom-call(f32[128,128]{1,0:T(8,128)S(1)} %convolution_subtract_fusion.17), custom_call_target="Cholesky" | custom-call | tf_op jit(solution)/shard_map/jit(cholesky)/cholesky | solution.py:104
  684.2 11.4 while.14
  684.9 2.2 bitcast_dynamic-update-slice_fusion.4
  687.7 2.2 bitcast_dynamic-update-slice_fusion.4
  690.6 2.2 bitcast_dynamic-update-slice_fusion.4
  695.6 39.3 %custom-call.38 = f32[4,128,128]{1,2,0:T(8,128)S(1)} custom-call(f32[4,128,128]{2,1,0:T(8,128)S(1)} %get-tuple-element.72), custom_call_target="InvertDiagBlocksLowerTriangular" | custom-call | tf_op jit(solution)/shard_map/triangular_solve/custom-call.3 | solution.py:105
  747.1 5.4 broadcast_select_fusion
  755.3 38.3 %reduce-scatter.9.cloned.1.call-done = f32[64,512]{1,0:T(8,128)} async-done(((f32[512,512]{1,0:T(8,128)}), f32[64,512]{1,0:T(8,128)}) %reduce-scatter.9.cloned.1.call-update) | async-done | bytes 131088 | tf_op jit(solution)/shard_map/reduce_scatter | solution.py:28
  793.7 40.9 %all-gather.8.cloned.1.call-done = f32[512,512]{1,0:T(8,128)} async-done(((f32[64,512]{1,0:T(8,128)}), f32[512,512]{1,0:T(8,128)}) %all-gather.8.cloned.1.call-update) | async-done | bytes 1048592 | tf_op jit(solution)/shard_map/all_gather | solution.py:29
  839.7 14.5 %all-reduce.3 = f32[512]{0:T(512)S(1)} all-reduce(f32[512]{0:T(512)S(1)} %slice_select_fusion.3), channel_id=4, replica_groups=mesh['row_0'=4,'row_1'=2,'col'=16] {'row_0','row_1'}, use_global_device_ids=true, to_apply=%region_18.22.clone | all-reduce | flops 512 | bytes 4096
  854.4 12.9 %all-reduce.1 = f32[512]{0:T(512)S(1)} all-reduce(f32[512]{0:T(512)S(1)} %dynamic-slice_dynamic-update-slice_fusion.1), channel_id=1, replica_groups=mesh['row_0'=4,'row_1'=2,'col'=16] {'row_0','row_1'}, use_global_device_ids=true, to_apply=%add.1 | all-reduce | flops 512 | bytes 4096
  868.7 2.4 fusion.68
  871.2 14.7 %all-reduce.4 = f32[512]{0:T(512)S(1)} all-reduce(f32[512]{0:T(512)S(1)} %slice_select_fusion.2), channel_id=5, replica_groups=mesh['row_0'=4,'row_1'=2,'col'=16] {'row_0','row_1'}, use_global_device_ids=true, to_apply=%region_19.24.clone | all-reduce | flops 512 | bytes 4096
  886.1 13.8 %all-reduce.2 = f32[512]{0:T(512)S(1)} all-reduce(f32[512]{0:T(512)S(1)} %dynamic-slice_dynamic-update-slice_fusion), channel_id=1, replica_groups=mesh['row_0'=4,'row_1'=2,'col'=16] {'row_0','row_1'}, use_global_device_ids=true, to_apply=%add.2 | all-reduce | flops 512 | bytes 4096
  899.9 89.2 %all-reduce.10.cloned.1.call-done = (f32[1024,512]{0,1:T(8,128)}, f32[512,512]{0,1:T(8,128)}) async-done(((f32[1024,512]{0,1:T(8,128)}, f32[512,512]{0,1:T(8,128)}), (f32[1024,512]{0,1:T(8,128)}, f32[512,512]{0,1:T(8,128)})) %all-reduce.10.cloned.1.call-update) | async-done | bytes 3145744 | tf_op jit(solution)/shard_map/psum | solution.py:34
  989.2 2.6 copy.49
  994.2 11.7 %cholesky.358 = f32[128,128]{1,0:T(8,128)S(1)} custom-call(f32[128,128]{1,0:T(8,128)S(1)} %cholesky.439), custom_call_target="Cholesky" | custom-call | tf_op jit(solution)/shard_map/jit(cholesky)/cholesky | solution.py:104
  1006.1 9.8 custom-call.40
  1018.4 11.7 %cholesky.377 = f32[128,128]{1,0:T(8,128)S(1)} custom-call(f32[128,128]{1,0:T(8,128)S(1)} %cholesky.443), custom_call_target="Cholesky" | custom-call | tf_op jit(solution)/shard_map/jit(cholesky)/cholesky | solution.py:104
  1031.5 10.0 custom-call.41
  1043.0 11.7 %cholesky.398 = f32[128,128]{1,0:T(8,128)S(1)} custom-call(f32[128,128]{1,0:T(8,128)S(1)} %cholesky.448), custom_call_target="Cholesky" | custom-call | tf_op jit(solution)/shard_map/jit(cholesky)/cholesky | solution.py:104
  1055.5 9.8 custom-call.42
  1066.8 11.7 %cholesky.415 = f32[128,128]{1,0:T(8,128)S(1)} custom-call(f32[128,128]{1,0:T(8,128)S(1)} %convolution_subtract_fusion.16), custom_call_target="Cholesky" | custom-call | tf_op jit(solution)/shard_map/jit(cholesky)/cholesky | solution.py:104
  1083.0 11.4 while.15
  1083.7 2.2 bitcast_dynamic-update-slice_fusion.5
  1094.4 39.3 %custom-call.43 = f32[4,128,128]{1,2,0:T(8,128)S(1)} custom-call(f32[4,128,128]{2,1,0:T(8,128)S(1)} %get-tuple-element.74), custom_call_target="InvertDiagBlocksLowerTriangular" | custom-call | tf_op jit(solution)/shard_map/triangular_solve/custom-call.3 | solution.py:105
  1151.3 5.3 convolution_subtract_fusion
  1156.6 2.9 copy.55
  (197 shorter events, 87.0 us)
Async XLA Ops:
  7.2 1.6 copy-start
  7.2 326.5 %all-gather.4.cloned.1.call-start = ((), (), s32[]{:S(2)}) async-start(), calls=%async_computation.4 | async-start | bytes 17825792 | tf_op jit(solution)/shard_map/all_gather | solution.py:78
  8.7 3.7 copy-start.19
  8.7 3.7 copy-start.20
  8.7 3.7 copy-start.21
  189.7 131.6 %all-to-all-start.1 = ((bf16[16,512,512]{2,1,0:T(8,128)(2,1)}), bf16[16,512,512]{2,1,0:T(8,128)(2,1)}, u32[]{:S(2)}, u32[]{:S(2)}) async-start(bf16[16,512,512]{2,1,0:T(8,128)(2,1)} %bitcast.254), calls=%async_computation.1 | async-start | bytes 16777216 | tf_op jit(solution)/shard_map/all_to_all | solution.py:82
  201.3 194.2 %reduce-scatter.7.cloned.1.call-start = ((), (), s32[]{:S(2)}) async-start(), calls=%async_computation.7 | async-start | bytes 1179648 | tf_op jit(solution)/shard_map/reduce_scatter | solution.py:28
  349.5 1.4 copy-start.6
  352.3 84.4 %all-gather.6.cloned.1.call-start = ((), (), s32[]{:S(2)}) async-start(), calls=%async_computation.5 | async-start | bytes 1179648 | tf_op jit(solution)/shard_map/all_gather | solution.py:29
  395.6 195.2 %all-reduce.12.cloned.1.call-start = ((), (), s32[]{:S(2)}) async-start(), calls=%async_computation.10 | async-start | bytes 6291456 | tf_op jit(solution)/shard_map/psum | solution.py:34
  439.4 354.3 %reduce-scatter.9.cloned.1.call-start = ((), (), s32[]{:S(2)}) async-start(), calls=%async_computation.8 | async-start | bytes 1179648 | tf_op jit(solution)/shard_map/reduce_scatter | solution.py:28
  590.7 2.6 copy-start.10
  594.8 1.0 copy-start.12
  695.6 43.5 %copy-start.4 = (f32[512,512]{1,0:T(8,128)S(1)}, f32[512,512]{1,0:T(8,128)}, u32[]{:S(2)}) copy-start(f32[512,512]{1,0:T(8,128)} %get-tuple-element.258) | copy-start | bytes 3145732
  735.0 4.2 copy-start.15
  740.5 6.6 copy-start.8
  742.3 4.8 copy-start.13
  743.3 3.8 copy-start.7
  752.4 1.4 copy-start.2
  755.3 79.3 %all-gather.8.cloned.1.call-start = ((), (), s32[]{:S(2)}) async-start(), calls=%async_computation.6 | async-start | bytes 1179648 | tf_op jit(solution)/shard_map/all_gather | solution.py:29
  793.6 195.5 %all-reduce.10.cloned.1.call-start = ((), (), s32[]{:S(2)}) async-start(), calls=%async_computation.9 | async-start | bytes 6291456 | tf_op jit(solution)/shard_map/psum | solution.py:34
  837.2 0.7 copy-start.18
  837.2 2.5 copy-start.16
  989.2 2.6 copy-start.9
  993.2 1.0 copy-start.11
  1136.2 5.8 copy-start.5
  1136.2 5.8 copy-start.14
  1147.5 3.8 copy-start.3
  1151.3 8.8 copy-start.1
  1159.5 0.6 copy-start.17
Sparse Core Ops, SparseCore 0:
  36.9 168.0 all-gather.3
  352.4 43.0 reduce-scatter.6
  397.2 39.4 all-gather.5
  439.7 151.0 all-reduce.11
  755.4 38.1 reduce-scatter.8
  795.1 39.4 all-gather.7
  837.7 151.3 all-reduce.9
